TPU v7x, 32 devices: a whole 2x2x4 slice. The times are simulated.
32 devices in a mesh: row: 8 (over z, core), col: 4 (over y, x).
Axes of the slice: x: 2, y: 2, z: 4, core: 2. Of those that a mesh axis runs over, the one named last changes fastest.
Arguments:
- loadings: bfloat16 [8, 32768, 1024], P(None, 'row', 'col'), may hold values from -6 to 6
- weights: bfloat16 [8, 32768, 512], P(None, 'row', 'col'), may hold values from -0.03125 to 0.03125
- specific: float32 [8, 32768], P(None, 'row'), may hold values from 0.2 to 5
- factor_cov: float32 [8, 1024, 1024], P(None, 'col'), may hold values from -0.001953125 to 0.0048828125, as said below
Outputs:
- portfolio_cov: float32 [8, 512, 512], P(None, 'row', 'col')
Inputs may be any that keep to these rules, and one draw needn't show every extreme that they name: `factor_cov`: each day's matrix is a symmetric positive definite factor covariance of order 1024.
All inputs are finite; a program needn't handle non-finite values.
Results may differ from a plain program's by a relative error of at most 0.0003.
Values may be sent and summed in bfloat16 or wider, within the bound.
A program may use at most 128 MiB of HBM per device.

v0:
```python
import functools

import jax
import jax.numpy as jnp
from jax import lax
from jax.experimental import pallas as pl
from jax.experimental.pallas import tpu as pltpu
from jax.sharding import PartitionSpec as P

F32, BF16 = jnp.float32, jnp.bfloat16
HIGHEST = lax.Precision.HIGHEST
CUTS, AHEAD = 4, 2
LAGS = (4, 5, 7, 9, 12, 15)


def by_dim(a, b, dim, precision=None):
    return lax.dot_general(
        a, b, (((dim,), (dim,)), ((), ())), precision=precision, preferred_element_type=F32
    )


def kernel(
    rows, cols, cuts, load_hbm, weight_hbm, spec_ref, fcov_hbm, out_ref,
    held, load, fcov, weighted, part, mate_in, pair, part_in, exp_rows, exp_cols, own_spec, prod, prod_in,
    w_sem, l_sem, f_sem, g_send, g_recv, m_send, m_recv, p_send, p_recv,
    er_send, er_recv, ec_send, ec_recv, q_send, q_recv,
):
    days, assets, factors = load_hbm.shape
    ports = weight_hbm.shape[2]
    slab = ports * cols // rows
    row, col = lax.axis_index("row"), lax.axis_index("col")
    near_x = col + 1 - 2 * (col % 2)
    near_y = (col + 2) % 4
    far = 3 - col
    chips, per = rows // 2, rows // cols
    piece = assets // cuts
    mine, core = row // 2, row % 2
    mate = row + 1 - 2 * core

    def to_row(r):
        return {"row": r, "col": col}

    def to_col(c):
        return {"row": row, "col": c}

    def remote(src, dst, send, recv, where):
        return pltpu.make_async_remote_copy(
            src_ref=src, dst_ref=dst, send_sem=send, recv_sem=recv,
            device_id=where, device_id_type=pl.DeviceIdType.MESH,
        )

    def lanes(buf, send, recv, d, u, start, size, lane, block):
        half = size // 2
        if lane == 2:
            size = half
        if lane == 3:
            start, size = start + half, half
        ref = buf.at[d, block, pl.ds(start, size)]
        where = near_x if lane in (0, 3) else near_y
        return remote(ref, ref, send.at[u, lane], recv.at[u, lane], to_col(where))

    def gather(u, lane, block):
        start = pl.multiple_of((u % cuts) * piece, piece)
        return lanes(held, g_send, g_recv, u // cuts, u, start, piece, lane, block)

    def exp_gather(d, lane, block):
        return lanes(exp_cols, ec_send, ec_recv, d, d, 0, slab, lane, block)

    def own_weights(d):
        return pltpu.make_async_copy(weight_hbm.at[d], held.at[d, col], w_sem.at[d])

    def get_load(d):
        return pltpu.make_async_copy(load_hbm.at[d], load.at[d % 2], l_sem.at[d % 2])

    def get_fcov(d):
        return pltpu.make_async_copy(fcov_hbm.at[d], fcov.at[d % 2], f_sem.at[d % 2])

    def mate_copy(d):
        return remote(
            part.at[d % 2, 1 - core], mate_in.at[d], m_send.at[d], m_recv.at[d], to_row(mate)
        )

    def part_copy(d, other, landed):
        return remote(
            pair.at[d % 2, other], part_in.at[d, landed],
            p_send.at[d, other], p_recv.at[d, landed], to_row(2 * other + core),
        )

    def exp_row_copy(d, slot, landed, other):
        ref = exp_rows.at[d, pl.ds(pl.multiple_of(landed * slab, slab), slab)]
        return remote(ref, ref, er_send.at[d, slot], er_recv.at[d, landed], to_row(other))

    def prod_copy(d, other, landed):
        return remote(
            prod.at[d, other], prod_in.at[d, landed],
            q_send.at[d, other], q_recv.at[d, landed], to_col(other),
        )

    def row_peers():
        return [(row + step) % rows for step in range(1, rows)]

    def chip_peers():
        return [(mine + step) % chips for step in range(1, chips)]

    def col_peers():
        return [near_x, near_y, far]

    def send_own(u):
        @pl.when(u % cuts == 0)
        def _():
            own_weights(u // cuts).wait()

        gather(u, 0, col).start()
        gather(u, 1, col).start()

    def pass_on(u):
        gather(u, 0, near_x).wait_recv()
        gather(u, 2, near_x).start()
        gather(u, 1, near_y).wait_recv()
        gather(u, 3, near_y).start()

    def sum_block(d, j):
        slot = d % 2
        lhs = held[d, j]
        by_factor = by_dim(lhs, load[slot], 0)
        by_port = by_dim(lhs, weighted[...], 0)
        for i in range(per):
            span = slice(i * slab, (i + 1) * slab)
            place = j * (per // 2) + i // 2
            part[slot, i % 2, place, :, pl.ds(0, factors)] = by_factor[span]
            part[slot, i % 2, place, :, pl.ds(factors, ports)] = by_port[span]

    def near_sums(d):
        scales = spec_ref[d]
        groups = scales.shape[0]
        copies = -(-128 // groups)
        tall = jnp.concatenate([scales] * copies, axis=0).T
        for i in range(groups):
            span = pl.ds(i * 128, 128)
            block = held[d, col, span].astype(F32) * tall[:, i : i + 1]
            weighted[span] = block.astype(BF16)

        @pl.when(d >= 2)
        def _():
            mate_copy(d - 2).wait_send()
            for peer in chip_peers():
                part_copy(d - 2, peer, mine).wait_send()

        get_load(d).wait()

        def near_block(i, carry):
            sum_block(d, (far + 1 + i) % cols)
            return carry

        lax.fori_loop(0, cols - 1, near_block, 0)

    def far_sums(d):
        slot = d % 2
        for q in range(cuts):
            gather(d * cuts + q, 2, far).wait_recv()
            gather(d * cuts + q, 3, far).wait_recv()
        sum_block(d, far)
        mate_copy(d).start()

        @pl.when(d + 2 < days)
        def _():
            get_load(d + 2).start()

        mate_copy(d).wait_recv()
        for peer in chip_peers():
            pair[slot, peer] = part[slot, core, peer] + mate_in[d, peer]
            part_copy(d, peer, mine).start()
        part_in[d, mine] = part[slot, core, mine] + mate_in[d, mine]

    def exposures(d):
        for peer in chip_peers():
            part_copy(d, mine, peer).wait_recv()
        total = part_in[d, 0]
        for z in range(1, chips):
            total = total + part_in[d, z]
        own_spec[d] = total[:, factors:]
        exp_rows[d, pl.ds(pl.multiple_of(row * slab, slab), slab)] = total[:, :factors]
        exp_cols[d, col] = total[:, :factors]
        exp_gather(d, 0, col).start()
        exp_gather(d, 1, col).start()
        for peer in chip_peers():
            exp_row_copy(d, 2 * peer + core, row, 2 * peer + core).start()
        exp_row_copy(d, mate, row, mate).start()

    def share(d):
        exp_gather(d, 0, near_x).wait_recv()
        exp_gather(d, 2, near_x).start()
        exp_gather(d, 1, near_y).wait_recv()
        exp_gather(d, 3, near_y).start()
        for peer in chip_peers():
            exp_row_copy(d, row, 2 * peer + core, mate).wait_recv()
            exp_row_copy(d, 2 * peer + 1 - core, 2 * peer + core, mate).start()

    def products(d):
        slot = d % 2
        get_fcov(d).wait()
        exp_gather(d, 2, far).wait_recv()
        exp_gather(d, 3, far).wait_recv()
        left = jnp.zeros((slab, factors), F32)
        for j in range(cols):
            left = left + by_dim(
                exp_cols[d, j], fcov[slot, :, pl.ds(j * factors, factors)], 1, HIGHEST
            )

        @pl.when(d + 2 < days)
        def _():
            get_fcov(d + 2).start()

        exp_row_copy(d, row, mate, mate).wait_recv()
        for peer in chip_peers():
            exp_row_copy(d, row, 2 * peer + 1 - core, mate).wait_recv()
        for j in range(cols):
            prod[d, j] = by_dim(left, exp_rows[d, pl.ds(j * ports, ports)], 1, HIGHEST)
        for peer in col_peers():
            prod_copy(d, peer, col).start()
        prod_in[d, col] = prod[d, col]

    def finish(d):
        for peer in col_peers():
            prod_copy(d, col, peer).wait_recv()
        total = own_spec[d]
        for j in range(cols):
            total = total + prod_in[d, j]
        out_ref[d] = total

    for d in range(days):
        own_weights(d).start()
    for d in range(min(2, days)):
        get_load(d).start()
        get_fcov(d).start()

    barrier = pltpu.get_barrier_semaphore()
    for peer in row_peers():
        pl.semaphore_signal(
            barrier, inc=1, device_id=to_row(peer), device_id_type=pl.DeviceIdType.MESH
        )
    for peer in col_peers():
        pl.semaphore_signal(
            barrier, inc=1, device_id=to_col(peer), device_id_type=pl.DeviceIdType.MESH
        )
    pl.semaphore_wait(barrier, rows + cols - 2)

    for u in range(AHEAD):
        send_own(u)

    def turn(t, carry):
        def stage(lag, what):
            @pl.when((t >= lag) & ((t - lag) % cuts == 0) & (t - lag < cuts * days))
            def _():
                what((t - lag) // cuts)

        @pl.when(t + AHEAD < cuts * days)
        def _():
            send_own(t + AHEAD)

        @pl.when(t < cuts * days)
        def _():
            pass_on(t)

        for lag, what in zip(LAGS, (near_sums, far_sums, exposures, share, products, finish)):
            stage(lag, what)
        return carry

    lax.fori_loop(0, cuts * (days - 1) + LAGS[-1] + 1, turn, 0)

    def drain(d, carry):
        for u in range(cuts):
            gather(d * cuts + u, 0, col).wait_send()
            gather(d * cuts + u, 1, col).wait_send()
            gather(d * cuts + u, 2, near_x).wait_send()
            gather(d * cuts + u, 3, near_y).wait_send()
        exp_gather(d, 0, col).wait_send()
        exp_gather(d, 1, col).wait_send()
        exp_gather(d, 2, near_x).wait_send()
        exp_gather(d, 3, near_y).wait_send()
        exp_row_copy(d, mate, row, mate).wait_send()
        for peer in chip_peers():
            exp_row_copy(d, 2 * peer + core, row, 2 * peer + core).wait_send()
            exp_row_copy(d, 2 * peer + 1 - core, 2 * peer + core, mate).wait_send()
        for peer in col_peers():
            prod_copy(d, peer, col).wait_send()

        @pl.when(d >= days - 2)
        def _():
            mate_copy(d).wait_send()
            for peer in chip_peers():
                part_copy(d, peer, mine).wait_send()

        return carry

    lax.fori_loop(0, days, drain, 0)


def fused(loadings, weights, specific, factor_cov):
    rows, cols = lax.axis_size("row"), lax.axis_size("col")
    days, assets, factors = loadings.shape
    ports = weights.shape[2]
    slab = ports * cols // rows
    scales = specific.reshape(days, assets // 128, 128)
    anywhere = pl.BlockSpec(memory_space=pl.ANY)
    inside = pl.BlockSpec(memory_space=pltpu.VMEM)
    dma = pltpu.SemaphoreType.DMA
    return pl.pallas_call(
        functools.partial(kernel, rows, cols, CUTS),
        out_shape=jax.ShapeDtypeStruct((days, slab, ports), F32),
        in_specs=[anywhere, anywhere, inside, anywhere],
        out_specs=inside,
        scratch_shapes=[
            pltpu.VMEM((days, cols, assets, ports), BF16),
            pltpu.VMEM((2, assets, factors), BF16),
            pltpu.VMEM((2, factors, cols * factors), F32),
            pltpu.VMEM((assets, ports), BF16),
            pltpu.VMEM((2, 2, rows // 2, slab, factors + ports), F32),
            pltpu.VMEM((days, rows // 2, slab, factors + ports), F32),
            pltpu.VMEM((2, rows // 2, slab, factors + ports), F32),
            pltpu.VMEM((days, rows // 2, slab, factors + ports), F32),
            pltpu.VMEM((days, cols * ports, factors), F32),
            pltpu.VMEM((days, cols, slab, factors), F32),
            pltpu.VMEM((days, slab, ports), F32),
            pltpu.VMEM((days, cols, slab, ports), F32),
            pltpu.VMEM((days, cols, slab, ports), F32),
            dma((days,)), dma((2,)), dma((2,)),
            dma((days * CUTS, 4)), dma((days * CUTS, 4)),
            dma((days,)), dma((days,)),
            dma((days, rows // 2)), dma((days, rows // 2)),
            dma((days, rows)), dma((days, rows)),
            dma((days, cols)), dma((days, cols)),
            dma((days, cols)), dma((days, cols)),
        ],
        compiler_params=pltpu.CompilerParams(
            collective_id=0, has_side_effects=True, vmem_limit_bytes=67_000_000
        ),
        name="covariance",
    )(loadings, weights, scales, factor_cov)


def plain(loadings, weights, specific, factor_cov):
    factor_cols = loadings.shape[2]
    port_cols = weights.shape[2]
    total_ports = port_cols * lax.axis_size("col")
    port_rows = total_ports // lax.axis_size("row")
    row_start = lax.axis_index("row") * port_rows
    weighted = (specific[:, :, None] * weights.astype(F32)).astype(BF16)
    fragment = lax.all_gather(weights, "col", axis=2, tiled=True)
    exposure_part = jnp.einsum("dar,dap->drp", loadings, fragment, preferred_element_type=F32)
    specific_term = jnp.einsum("dak,dap->dkp", weighted, fragment, preferred_element_type=F32)
    joined = jnp.concatenate([exposure_part, specific_term], axis=1)
    exposure = lax.psum(joined[:, :factor_cols, :], "row")
    specific_block = lax.psum_scatter(
        joined[:, factor_cols:, :], "row", scatter_dimension=2, tiled=True
    )
    exposure_rows = lax.dynamic_slice_in_dim(exposure, row_start, port_rows, 2)
    left_part = jnp.einsum("dri,drs->dis", exposure_rows, factor_cov, precision=HIGHEST)
    left = lax.psum(left_part, "col")
    exposure_cols = lax.all_to_all(exposure, "col", split_axis=2, concat_axis=1, tiled=True)
    factor_block = jnp.einsum("dir,drk->dik", left, exposure_cols, precision=HIGHEST)
    return factor_block + jnp.swapaxes(specific_block, 1, 2)


def solution(mesh):
    in_specs = (P(None, "row", "col"), P(None, "row", "col"), P(None, "row"), P(None, "col", None))
    out_specs = P(None, "row", "col")
    rows, cols = mesh.shape["row"], mesh.shape["col"]
    body = fused if cols == 4 and rows % (2 * cols) == 0 else plain
    return jax.shard_map(body, mesh=mesh, in_specs=in_specs, out_specs=out_specs, check_vma=False)
```

profile of v0, /device:TPU:0, one launch (start us, length us, event | category | flops | bytes accessed | tf_op | source)
XLA Modules:
  0.0 330.7 jit_solution(6472951391445066049)
XLA Ops:
  0.0 1.6 copy.7
  1.6 327.4 %covariance.1 = f32[8,64,128]{2,1,0:T(8,128)} custom-call(bf16[8,4096,256]{2,1,0:T(8,128)(2,1)} %load_hbm.1, bf16[8,4096,128]{2,1,0:T(8,128)(2,1)} %weight_hbm.1, f32[8,32,128]{2,1,0:T(8,128)} %bitcast.4, f32[8,256,1024]{2,1,0:T(8,128)} %fcov_hbm.1), custom_call_target="tpu_custom_call" | custom-call | tf_op jit(solution)/shard_map/covariance/pallas_call | solution.py:308
  329.0 1.7 copy.9
where the time goes:
time: 331 us
  Pallas kernels  327 us (99%)
    pallas_call x1, Pallas kernels, fused(): pl.pallas_call(functools.partial(kernel, rows, cols, CUTS), out_shape=jax...  327 us

commit v1 on v0

v1 whole, which is shorter than its diff:
```python
import functools

import jax
import jax.numpy as jnp
from jax import lax
from jax.experimental import pallas as pl
from jax.experimental.pallas import tpu as pltpu
from jax.sharding import PartitionSpec as P

F32, BF16 = jnp.float32, jnp.bfloat16
HIGHEST = lax.Precision.HIGHEST
CUTS, AHEAD, EXTRA = 4, 2, 1
LAGS = (4, 5, 5, 6, 9, 11, 13, 16, 19)
GIVEN = (((0, 0), (0, 1), (0, 2)), ((0, 3), (1, 0)), ((1, 1),), ((1, 2), (1, 3)))


def by_dim(a, b, dim, precision=None):
    return lax.dot_general(
        a, b, (((dim,), (dim,)), ((), ())), precision=precision, preferred_element_type=F32
    )


def kernel(
    rows, cols, cuts, load_hbm, weight_hbm, spec_ref, fcov_hbm, out_ref,
    held, load, load_in, fcov, weighted, part, mate_in, pair, part_in, swap, swap_in,
    exp_rows, exp_cols, own_spec, prod, prod_in,
    w_sem, l_sem, f_sem, g_send, g_recv, m_send, m_recv, p_send, p_recv, s_send, s_recv,
    er_send, er_recv, ec_send, ec_recv, q_send, q_recv,
):
    days, assets, factors = load_hbm.shape
    ports = weight_hbm.shape[2]
    slab = ports * cols // rows
    row, col = lax.axis_index("row"), lax.axis_index("col")
    near_x = col + 1 - 2 * (col % 2)
    near_y = (col + 2) % 4
    far = 3 - col
    chips, per = rows // 2, rows // cols
    half = assets // 2
    piece = half // cuts
    mine, core = row // 2, row % 2
    spans = (pl.ds(0, factors), pl.ds(factors, factors), pl.ds(2 * factors, 2 * ports))
    mate = row + 1 - 2 * core

    def merger(d):
        return near_x + (d % 2) * (near_y - near_x)

    def other(d):
        return near_y + (d % 2) * (near_x - near_y)

    def side(d):
        return col % 2 + (d % 2) * (col // 2 - col % 2)

    def to_row(r):
        return {"row": r, "col": col}

    def to_col(c):
        return {"row": row, "col": c}

    def remote(src, dst, send, recv, where):
        return pltpu.make_async_remote_copy(
            src_ref=src, dst_ref=dst, send_sem=send, recv_sem=recv,
            device_id=where, device_id_type=pl.DeviceIdType.MESH,
        )

    def kept(d, start, size):
        return pl.ds(pl.multiple_of(side(d) * half + start, piece), size)

    def given(d, start, size):
        return pl.ds(pl.multiple_of((1 - side(d)) * half + start, piece), size)

    def gather(u, lane, block):
        d, start = u // cuts, pl.multiple_of((u % cuts) * piece, piece)
        if lane == 1:
            dst = load_in.at[d, pl.ds(start, piece)]
            src = load_hbm.at[d, given(d, start, piece)]
        else:
            dst = held.at[d, block, pl.ds(start, piece)]
            src = dst
        if lane == 0:
            src = weight_hbm.at[d, given(d, start, piece)]
        if lane == 2:
            src = weight_hbm.at[d, kept(d, start, piece)]
        where = merger(d) if lane < 2 else other(d)
        return remote(src, dst, g_send.at[u, lane], g_recv.at[u, lane], to_col(where))

    def own_weights(d):
        return pltpu.make_async_copy(
            weight_hbm.at[d, kept(d, 0, half)], held.at[d, col], w_sem.at[d]
        )

    def get_load(d):
        return pltpu.make_async_copy(
            load_hbm.at[d, kept(d, 0, half)], load.at[d % 2], l_sem.at[d % 2]
        )

    def get_fcov(d):
        return pltpu.make_async_copy(fcov_hbm.at[d], fcov.at[d % 2], f_sem.at[d % 2])

    def mate_copy(d, lane):
        span = spans[lane]
        return remote(
            part.at[d % 2, 1 - core, :, :, span], mate_in.at[d, :, :, span],
            m_send.at[d, lane], m_recv.at[d, lane], to_row(mate),
        )

    def part_copy(d, lane, other_chip, landed):
        span = spans[lane]
        return remote(
            pair.at[d % 2, other_chip, :, span], part_in.at[d, landed, :, span],
            p_send.at[d, lane, other_chip], p_recv.at[d, lane, landed],
            to_row(2 * other_chip + core),
        )

    def summed(d, lane):
        for peer in chip_peers():
            part_copy(d, lane, mine, peer).wait_recv()
        total = part_in[d, 0, :, spans[lane]]
        for z in range(1, chips):
            total = total + part_in[d, z, :, spans[lane]]
        return total

    def swap_copy(d):
        return remote(
            swap.at[d], swap_in.at[d], s_send.at[d], s_recv.at[d], to_col(merger(d))
        )

    def exp_gather(d, lane, block):
        start, size = (slab // 2 if lane == 3 else 0), (slab if lane < 2 else slab // 2)
        ref = exp_cols.at[d, block, pl.ds(start, size)]
        where = near_x if lane in (0, 3) else near_y
        return remote(ref, ref, ec_send.at[d, lane], ec_recv.at[d, lane], to_col(where))

    def exp_row_copy(d, slot, landed, other_row):
        ref = exp_rows.at[d, pl.ds(pl.multiple_of(landed * slab, slab), slab)]
        return remote(ref, ref, er_send.at[d, slot], er_recv.at[d, landed], to_row(other_row))

    def prod_copy(d, other_col, landed):
        return remote(
            prod.at[d, other_col], prod_in.at[d, landed],
            q_send.at[d, other_col], q_recv.at[d, landed], to_col(other_col),
        )

    def row_peers():
        return [(row + step) % rows for step in range(1, rows)]

    def chip_peers():
        return [(mine + step) % chips for step in range(1, chips)]

    def col_peers():
        return [near_x, near_y, far]

    def exchange_own(u):
        gather(u, 2, col).start()

    def donate(u):
        first = u - u % cuts
        for q, parts in enumerate(GIVEN):
            @pl.when(u % cuts == q)
            def _(parts=parts):
                for lane, part_of_day in parts:
                    gather(first + part_of_day, lane, col).start()

    def pass_on(u):
        block = merger(u // cuts)

        @pl.when(u % cuts < cuts // 2)
        def _():
            for step in range(2):
                chunk = u + u % cuts + step
                gather(chunk, 0, block).wait_recv()
                gather(chunk, 3, block).start()

    def store(slot, j, lane, values):
        for i in range(per):
            place = j * (per // 2) + i // 2
            part[slot, i % 2, place, :, pl.ds(lane, values.shape[1])] = (
                values[i * slab : (i + 1) * slab]
            )

    def sum_own(d, j):
        slot = d % 2
        lhs = held[d, j]
        store(slot, j, factors, by_dim(lhs, load[slot], 0))
        store(slot, j, 2 * factors, by_dim(lhs, weighted[...], 0))

    def own_sums(d):
        for q in range(cuts):
            gather(d * cuts + q, 2, other(d)).wait_recv()
            gather(d * cuts + q, 3, far).wait_recv()
        own_weights(d).wait()
        groups = half // 128
        scales = spec_ref[d, pl.ds(pl.multiple_of(side(d) * groups, groups), groups)]
        copies = -(-128 // groups)
        tall = jnp.concatenate([scales] * copies, axis=0).T
        for i in range(groups):
            span = pl.ds(i * 128, 128)
            for lane, block in enumerate((col, merger(d))):
                scaled = held[d, block, span].astype(F32) * tall[:, i : i + 1]
                weighted[span, pl.ds(lane * ports, ports)] = scaled.astype(BF16)

        @pl.when(d >= 2)
        def _():
            for lane in range(3):
                mate_copy(d - 2, lane).wait_send()
                for peer in chip_peers():
                    part_copy(d - 2, lane, peer, mine).wait_send()

        get_load(d).wait()

        def own_block(j, carry):
            sum_own(d, j)
            return carry

        lax.fori_loop(0, cols, own_block, 0)
        mate_copy(d, 1).start()
        mate_copy(d, 2).start()

        @pl.when(d + 2 < days)
        def _():
            get_load(d + 2).start()

    def merged_sums(d):
        for q in range(cuts):
            gather(d * cuts + q, 1, col).wait_recv()

        def merged_block(j, carry):
            store(d % 2, j, 0, by_dim(held[d, j], load_in[d], 0))
            return carry

        lax.fori_loop(0, cols, merged_block, 0)
        mate_copy(d, 0).start()

    def pair_up(d, lane):
        slot, span = d % 2, spans[lane]
        mate_copy(d, lane).wait_recv()
        for peer in chip_peers():
            pair[slot, peer, :, span] = part[slot, core, peer, :, span] + mate_in[d, peer, :, span]
            part_copy(d, lane, peer, mine).start()
        part_in[d, mine, :, span] = part[slot, core, mine, :, span] + mate_in[d, mine, :, span]

    def pair_own(d):
        pair_up(d, 1)

    def pair_merged(d):
        pair_up(d, 0)

    def trade(d):
        swap[d] = summed(d, 0)
        swap_copy(d).start()

    def exposures(d):
        total = summed(d, 1)
        swap_copy(d).wait_recv()
        own = total + swap_in[d]
        exp_cols[d, col] = own
        exp_rows[d, pl.ds(pl.multiple_of(row * slab, slab), slab)] = own
        for peer in chip_peers():
            exp_row_copy(d, 2 * peer + core, row, 2 * peer + core).start()
        exp_gather(d, 0, col).start()
        exp_gather(d, 1, col).start()
        exp_row_copy(d, mate, row, mate).start()
        pair_up(d, 2)

    def share(d):
        exp_gather(d, 0, near_x).wait_recv()
        exp_gather(d, 2, near_x).start()
        exp_gather(d, 1, near_y).wait_recv()
        exp_gather(d, 3, near_y).start()
        for peer in chip_peers():
            exp_row_copy(d, row, 2 * peer + core, mate).wait_recv()
            exp_row_copy(d, 2 * peer + 1 - core, 2 * peer + core, mate).start()

    def products(d):
        slot = d % 2
        get_fcov(d).wait()
        exp_gather(d, 2, far).wait_recv()
        exp_gather(d, 3, far).wait_recv()
        left = jnp.zeros((slab, factors), F32)
        for j in range(cols):
            left = left + by_dim(
                exp_cols[d, j], fcov[slot, :, pl.ds(j * factors, factors)], 1, HIGHEST
            )

        @pl.when(d + 2 < days)
        def _():
            get_fcov(d + 2).start()

        exp_row_copy(d, row, mate, mate).wait_recv()
        for peer in chip_peers():
            exp_row_copy(d, row, 2 * peer + 1 - core, mate).wait_recv()
        for j in range(cols):
            prod[d, j] = by_dim(left, exp_rows[d, pl.ds(j * ports, ports)], 1, HIGHEST)
        block = merger(d)
        total = summed(d, 2)
        own_spec[d] = total[:, :ports]
        prod[d, block] = prod[d, block] + total[:, ports:]
        for peer in col_peers():
            prod_copy(d, peer, col).start()
        prod_in[d, col] = prod[d, col]

    def finish(d):
        for peer in col_peers():
            prod_copy(d, col, peer).wait_recv()
        total = own_spec[d]
        for j in range(cols):
            total = total + prod_in[d, j]
        out_ref[d] = total

    barrier = pltpu.get_barrier_semaphore()
    for peer in row_peers():
        pl.semaphore_signal(
            barrier, inc=1, device_id=to_row(peer), device_id_type=pl.DeviceIdType.MESH
        )
    for peer in col_peers():
        pl.semaphore_signal(
            barrier, inc=1, device_id=to_col(peer), device_id_type=pl.DeviceIdType.MESH
        )
    for d in range(days):
        own_weights(d).start()
    for d in range(min(2, days)):
        get_load(d).start()
        get_fcov(d).start()
    pl.semaphore_wait(barrier, rows + cols - 2)

    units = cuts * days
    for u in range(AHEAD):
        exchange_own(u)
    for u in range(AHEAD + EXTRA):
        if u < AHEAD or (u // cuts) % 2 == 1:
            donate(u)

    def turn(t, carry):
        def stage(lag, what):
            @pl.when((t >= lag) & ((t - lag) % cuts == 0) & (t - lag < units))
            def _():
                what((t - lag) // cuts)

        soon, later = t + AHEAD, t + AHEAD + EXTRA

        @pl.when((soon < units) & ((soon // cuts) % 2 == 0))
        def _():
            donate(soon)

        @pl.when(soon < units)
        def _():
            exchange_own(soon)

        @pl.when((later < units) & ((later // cuts) % 2 == 1))
        def _():
            donate(later)

        @pl.when(t < units)
        def _():
            pass_on(t)

        for lag, what in zip(
            LAGS, (own_sums, pair_own, merged_sums, pair_merged, trade, exposures, share, products, finish)
        ):
            stage(lag, what)
        return carry

    lax.fori_loop(0, cuts * (days - 1) + LAGS[-1] + 1, turn, 0)

    def drain(d, carry):
        for q in range(cuts):
            u = d * cuts + q
            gather(u, 0, col).wait_send()
            gather(u, 1, col).wait_send()
            gather(u, 2, col).wait_send()
            gather(u, 3, merger(d)).wait_send()
        swap_copy(d).wait_send()
        exp_gather(d, 0, col).wait_send()
        exp_gather(d, 1, col).wait_send()
        exp_gather(d, 2, near_x).wait_send()
        exp_gather(d, 3, near_y).wait_send()
        exp_row_copy(d, mate, row, mate).wait_send()
        for peer in chip_peers():
            exp_row_copy(d, 2 * peer + core, row, 2 * peer + core).wait_send()
            exp_row_copy(d, 2 * peer + 1 - core, 2 * peer + core, mate).wait_send()
        for peer in col_peers():
            prod_copy(d, peer, col).wait_send()

        @pl.when(d >= days - 2)
        def _():
            for lane in range(3):
                mate_copy(d, lane).wait_send()
                for peer in chip_peers():
                    part_copy(d, lane, peer, mine).wait_send()

        return carry

    lax.fori_loop(0, days, drain, 0)


def fused(loadings, weights, specific, factor_cov):
    rows, cols = lax.axis_size("row"), lax.axis_size("col")
    days, assets, factors = loadings.shape
    ports = weights.shape[2]
    slab = ports * cols // rows
    half, wide = assets // 2, 2 * (factors + ports)
    scales = specific.reshape(days, assets // 128, 128)
    anywhere = pl.BlockSpec(memory_space=pl.ANY)
    inside = pl.BlockSpec(memory_space=pltpu.VMEM)
    dma = pltpu.SemaphoreType.DMA
    return pl.pallas_call(
        functools.partial(kernel, rows, cols, CUTS),
        out_shape=jax.ShapeDtypeStruct((days, slab, ports), F32),
        in_specs=[anywhere, anywhere, inside, anywhere],
        out_specs=inside,
        scratch_shapes=[
            pltpu.VMEM((days, cols, half, ports), BF16),
            pltpu.VMEM((2, half, factors), BF16),
            pltpu.VMEM((days, half, factors), BF16),
            pltpu.VMEM((2, factors, cols * factors), F32),
            pltpu.VMEM((half, 2 * ports), BF16),
            pltpu.VMEM((2, 2, rows // 2, slab, wide), F32),
            pltpu.VMEM((days, rows // 2, slab, wide), F32),
            pltpu.VMEM((2, rows // 2, slab, wide), F32),
            pltpu.VMEM((days, rows // 2, slab, wide), F32),
            pltpu.VMEM((days, slab, factors), F32),
            pltpu.VMEM((days, slab, factors), F32),
            pltpu.VMEM((days, cols * ports, factors), F32),
            pltpu.VMEM((days, cols, slab, factors), F32),
            pltpu.VMEM((days, slab, ports), F32),
            pltpu.VMEM((days, cols, slab, ports), F32),
            pltpu.VMEM((days, cols, slab, ports), F32),
            dma((days,)), dma((2,)), dma((2,)),
            dma((days * CUTS, 4)), dma((days * CUTS, 4)),
            dma((days, 3)), dma((days, 3)),
            dma((days, 3, rows // 2)), dma((days, 3, rows // 2)),
            dma((days,)), dma((days,)),
            dma((days, rows)), dma((days, rows)),
            dma((days, 4)), dma((days, 4)),
            dma((days, cols)), dma((days, cols)),
        ],
        compiler_params=pltpu.CompilerParams(
            collective_id=0, has_side_effects=True, vmem_limit_bytes=67_000_000
        ),
        name="covariance",
    )(loadings, weights, scales, factor_cov)


def plain(loadings, weights, specific, factor_cov):
    factor_cols = loadings.shape[2]
    port_cols = weights.shape[2]
    total_ports = port_cols * lax.axis_size("col")
    port_rows = total_ports // lax.axis_size("row")
    row_start = lax.axis_index("row") * port_rows
    weighted = (specific[:, :, None] * weights.astype(F32)).astype(BF16)
    fragment = lax.all_gather(weights, "col", axis=2, tiled=True)
    exposure_part = jnp.einsum("dar,dap->drp", loadings, fragment, preferred_element_type=F32)
    specific_term = jnp.einsum("dak,dap->dkp", weighted, fragment, preferred_element_type=F32)
    joined = jnp.concatenate([exposure_part, specific_term], axis=1)
    exposure = lax.psum(joined[:, :factor_cols, :], "row")
    specific_block = lax.psum_scatter(
        joined[:, factor_cols:, :], "row", scatter_dimension=2, tiled=True
    )
    exposure_rows = lax.dynamic_slice_in_dim(exposure, row_start, port_rows, 2)
    left_part = jnp.einsum("dri,drs->dis", exposure_rows, factor_cov, precision=HIGHEST)
    left = lax.psum(left_part, "col")
    exposure_cols = lax.all_to_all(exposure, "col", split_axis=2, concat_axis=1, tiled=True)
    factor_block = jnp.einsum("dir,drk->dik", left, exposure_cols, precision=HIGHEST)
    return factor_block + jnp.swapaxes(specific_block, 1, 2)


def solution(mesh):
    in_specs = (P(None, "row", "col"), P(None, "row", "col"), P(None, "row"), P(None, "col", None))
    out_specs = P(None, "row", "col")
    rows, cols = mesh.shape["row"], mesh.shape["col"]
    body = fused if cols == 4 and rows % (2 * cols) == 0 else plain
    return jax.shard_map(body, mesh=mesh, in_specs=in_specs, out_specs=out_specs, check_vma=False)
```

time: 331 us -> 318 us (0.961)
  Pallas kernels: 327 us -> 313 us
    pallas_call x1, Pallas kernels: 327 us -> 313 us  [fused(): pl.pallas_call(functools.partial(kernel, rows, cols, CUTS), out_shape=jax...]
where the time goes in v1:
time: 318 us; the launch traced here: 316 us
  Pallas kernels  313 us (98%)
  local copies, waits for them, and re-layouts  3.26 us (1%)
    pallas_call x1, Pallas kernels, fused(): pl.pallas_call(functools.partial(kernel, rows, cols, CUTS), out_shape=jax...  313 us

profile of v1, /device:TPU:0, one launch (start us, length us, event | category | flops | bytes accessed | tf_op | source)
XLA Modules:
  0.0 316.2 jit_solution(14454076287140033881)
XLA Ops:
  0.0 1.6 copy.7
  1.6 313.0 %covariance.1 = f32[8,64,128]{2,1,0:T(8,128)} custom-call(bf16[8,4096,256]{2,1,0:T(8,128)(2,1)} %load_hbm.1, bf16[8,4096,128]{2,1,0:T(8,128)(2,1)} %weight_hbm.1, f32[8,32,128]{2,1,0:T(8,128)} %bitcast.4, f32[8,256,1024]{2,1,0:T(8,128)} %fcov_hbm.1), custom_call_target="tpu_custom_call" | custom-call | tf_op jit(solution)/shard_map/covariance/pallas_call | solution.py:405
  314.6 1.7 copy.9

commit v2 on v1

--- a/solution.py
+++ b/solution.py
@@ -9,7 +9,7 @@
 
 F32, BF16 = jnp.float32, jnp.bfloat16
 HIGHEST = lax.Precision.HIGHEST
-CUTS, AHEAD, EXTRA = 4, 2, 1
+CUTS, AHEAD, EXTRA = 4, 2, 0
 LAGS = (4, 5, 5, 6, 9, 11, 13, 16, 19)
 GIVEN = (((0, 0), (0, 1), (0, 2)), ((0, 3), (1, 0)), ((1, 1),), ((1, 2), (1, 3)))
 
@@ -22,7 +22,7 @@
 
 def kernel(
     rows, cols, cuts, load_hbm, weight_hbm, spec_ref, fcov_hbm, out_ref,
-    held, load, load_in, fcov, weighted, part, mate_in, pair, part_in, swap, swap_in,
+    scale_rows, held, load, load_in, fcov, weighted, part, mate_in, pair, part_in, swap, swap_in,
     exp_rows, exp_cols, own_spec, prod, prod_in,
     w_sem, l_sem, f_sem, g_send, g_recv, m_send, m_recv, p_send, p_recv, s_send, s_recv,
     er_send, er_recv, ec_send, ec_recv, q_send, q_recv,
@@ -189,7 +189,7 @@
             gather(d * cuts + q, 3, far).wait_recv()
         own_weights(d).wait()
         groups = half // 128
-        scales = spec_ref[d, pl.ds(pl.multiple_of(side(d) * groups, groups), groups)]
+        scales = scale_rows[d, pl.ds(pl.multiple_of(side(d) * groups, groups), groups)]
         copies = -(-128 // groups)
         tall = jnp.concatenate([scales] * copies, axis=0).T
         for i in range(groups):
@@ -240,6 +240,7 @@
 
     def pair_own(d):
         pair_up(d, 1)
+        pair_up(d, 2)
 
     def pair_merged(d):
         pair_up(d, 0)
@@ -259,7 +260,6 @@
         exp_gather(d, 0, col).start()
         exp_gather(d, 1, col).start()
         exp_row_copy(d, mate, row, mate).start()
-        pair_up(d, 2)
 
     def share(d):
         exp_gather(d, 0, near_x).wait_recv()
@@ -285,14 +285,18 @@
         def _():
             get_fcov(d + 2).start()
 
+        def product(j):
+            block = exp_rows[d, pl.ds(pl.multiple_of(j * ports, ports), ports)]
+            return by_dim(left, block, 1, HIGHEST)
+
         exp_row_copy(d, row, mate, mate).wait_recv()
+        prod[d, mine] = product(mine)
         for peer in chip_peers():
             exp_row_copy(d, row, 2 * peer + 1 - core, mate).wait_recv()
-        for j in range(cols):
-            prod[d, j] = by_dim(left, exp_rows[d, pl.ds(j * ports, ports)], 1, HIGHEST)
-        block = merger(d)
+            prod[d, peer] = product(peer)
         total = summed(d, 2)
         own_spec[d] = total[:, :ports]
+        block = merger(d)
         prod[d, block] = prod[d, block] + total[:, ports:]
         for peer in col_peers():
             prod_copy(d, peer, col).start()
@@ -328,6 +332,9 @@
     for u in range(AHEAD + EXTRA):
         if u < AHEAD or (u // cuts) % 2 == 1:
             donate(u)
+
+    for i in range(assets // 128):
+        scale_rows[:, i, :] = spec_ref[:, pl.ds(i * 128, 128)]
 
     def turn(t, carry):
         def stage(lag, what):
@@ -398,7 +405,6 @@
     ports = weights.shape[2]
     slab = ports * cols // rows
     half, wide = assets // 2, 2 * (factors + ports)
-    scales = specific.reshape(days, assets // 128, 128)
     anywhere = pl.BlockSpec(memory_space=pl.ANY)
     inside = pl.BlockSpec(memory_space=pltpu.VMEM)
     dma = pltpu.SemaphoreType.DMA
@@ -408,6 +414,7 @@
         in_specs=[anywhere, anywhere, inside, anywhere],
         out_specs=inside,
         scratch_shapes=[
+            pltpu.VMEM((days, assets // 128, 128), F32),
             pltpu.VMEM((days, cols, half, ports), BF16),
             pltpu.VMEM((2, half, factors), BF16),
             pltpu.VMEM((days, half, factors), BF16),
@@ -437,7 +444,7 @@
             collective_id=0, has_side_effects=True, vmem_limit_bytes=67_000_000
         ),
         name="covariance",
-    )(loadings, weights, scales, factor_cov)
+    )(loadings, weights, specific, factor_cov)
 
 
 def plain(loadings, weights, specific, factor_cov):
@@ -467,5 +474,5 @@
     in_specs = (P(None, "row", "col"), P(None, "row", "col"), P(None, "row"), P(None, "col", None))
     out_specs = P(None, "row", "col")
     rows, cols = mesh.shape["row"], mesh.shape["col"]
-    body = fused if cols == 4 and rows % (2 * cols) == 0 else plain
+    body = fused if cols == 4 and rows == 2 * cols else plain
     return jax.shard_map(body, mesh=mesh, in_specs=in_specs, out_specs=out_specs, check_vma=False)

time: 318 us -> 306 us (0.962)
  Pallas kernels: 313 us -> 304 us
    pallas_call x1, Pallas kernels: 313 us -> 304 us  [fused(): pl.pallas_call(functools.partial(kernel, rows, cols, CUTS), out_shape=jax...]
where the time goes in v2:
time: 306 us
  Pallas kernels  304 us (99%)
    pallas_call x1, Pallas kernels, fused(): pl.pallas_call(functools.partial(kernel, rows, cols, CUTS), out_shape=jax...  304 us

profile of v2, /device:TPU:0, one launch (start us, length us, event | category | flops | bytes accessed | tf_op | source)
XLA Modules:
  0.0 306.1 jit_solution(10035262800541114512)
XLA Ops:
  0.0 304.4 %covariance.1 = f32[8,64,128]{2,1,0:T(8,128)} custom-call(bf16[8,4096,256]{2,1,0:T(8,128)(2,1)} %load_hbm.1, bf16[8,4096,128]{2,1,0:T(8,128)(2,1)} %weight_hbm.1, f32[8,4096]{1,0:T(8,128)} %spec_ref.1, f32[8,256,1024]{2,1,0:T(8,128)} %fcov_hbm.1), custom_call_target="tpu_custom_call" | custom-call | tf_op jit(solution)/shard_map/covariance/pallas_call | solution.py:411
  304.4 1.7 copy.6

commit v3 on v2

--- a/solution.py
+++ b/solution.py
@@ -9,8 +9,8 @@
 
 F32, BF16 = jnp.float32, jnp.bfloat16
 HIGHEST = lax.Precision.HIGHEST
-CUTS, AHEAD, EXTRA = 4, 2, 0
-LAGS = (4, 5, 5, 6, 9, 11, 13, 16, 19)
+CUTS, AHEAD, EXTRA = 4, 1, 0
+LAGS = (4, 5, 5, 6, 8, 10, 12, 14, 16)
 GIVEN = (((0, 0), (0, 1), (0, 2)), ((0, 3), (1, 0)), ((1, 1),), ((1, 2), (1, 3)))
 
 

time: 306 us -> 305 us (level)
  no operation moved by 1% of the time
where the time goes in v3:
time: 305 us
  Pallas kernels  304 us (100%)
    pallas_call x1, Pallas kernels, fused(): pl.pallas_call(functools.partial(kernel, rows, cols, CUTS), out_shape=jax...  304 us

profile of v3, /device:TPU:0, one launch (start us, length us, event | category | flops | bytes accessed | tf_op | source)
XLA Modules:
  0.0 305.3 jit_solution(12287461722889985360)
XLA Ops:
  0.0 303.6 %covariance.1 = f32[8,64,128]{2,1,0:T(8,128)} custom-call(bf16[8,4096,256]{2,1,0:T(8,128)(2,1)} %load_hbm.1, bf16[8,4096,128]{2,1,0:T(8,128)(2,1)} %weight_hbm.1, f32[8,4096]{1,0:T(8,128)} %spec_ref.1, f32[8,256,1024]{2,1,0:T(8,128)} %fcov_hbm.1), custom_call_target="tpu_custom_call" | custom-call | tf_op jit(solution)/shard_map/covariance/pallas_call | solution.py:411
  303.6 1.7 copy.6
